TPU v7x, 32 devices: a whole 2x2x4 slice. The times are simulated.
32 devices in a mesh: groups: 2 (over x), seq: 16 (over z, y, core).
Axes of the slice: x: 2, y: 2, z: 4, core: 2. Of those that a mesh axis runs over, the one named last changes fastest.
Arguments:
- self_query: bfloat16 [16, 8192], P('groups'), parts along dimension 0, may hold values from -128 to 128
- new_key: bfloat16 [16, 8192], P('groups'), parts along dimension 0, may hold values from -6 to 6
- new_value: bfloat16 [16, 8192], P('groups'), parts along dimension 0, may hold values from -12 to 12
- cache_keys: bfloat16 [16, 1024, 8192], P('groups', 'seq'), parts along dimension 0, may hold values from -8 to 8
- cache_values: bfloat16 [16, 1024, 8192], P('groups', 'seq'), parts along dimension 0, may hold values from -12 to 12
- lengths: int32 [16], P('groups'), parts along dimension 0, may hold values from 128 to 1024
- db_keys: bfloat16 [32, 128, 8192], P(('groups', 'seq')), parts along dimension 0, may hold values from -8 to 8
- db_values: bfloat16 [32, 128, 8192], P(('groups', 'seq')), parts along dimension 0, may hold values from -12 to 12
- cross_query: bfloat16 [16, 8192], P('groups'), parts along dimension 0, may hold values from -128 to 128
- neighbour_ids: int32 [16, 2], P('groups'), parts along dimension 0, may hold values from 0 to 15
Outputs:
- self_out: bfloat16 [16, 8192], P('groups', 'seq'), parts along dimension 0
- cross_out: bfloat16 [16, 8192], P('groups', 'seq'), parts along dimension 0
There are 2 independent parts, one for each index of `groups`. A program takes and returns all parts, laid end to end along the dimension named above; each array names one. Nothing has to cross between parts.
Inputs may be any that keep to these rules, and one draw needn't show every extreme that they name: `neighbour_ids`: the 2 ids of a row may repeat.
All inputs are finite; a program needn't handle non-finite values.
Results may differ from a plain program's by a relative error of at most 0.022.
Values may be sent and summed in bfloat16 or wider, within the bound.
A program may use at most 64 MiB of HBM per device.

v0:
```python
import jax
import jax.numpy as jnp
from jax import lax
from jax.sharding import PartitionSpec as P

DH = 128


NEG = -1e30


def joined_2(shard, axis, combine):
    everything = jax.tree.map(lambda part: lax.all_gather(part, axis), shard)
    initial = jax.tree.map(lambda part: part[0], everything)

    def turn(k, so_far):
        return combine(so_far, jax.tree.map(lambda part: part[k], everything))

    return lax.fori_loop(1, lax.axis_size(axis), turn, initial)


def blend(first, second):
    peak_a, den_a, acc_a = first
    peak_b, den_b, acc_b = second
    peak = jnp.maximum(peak_a, peak_b)
    factor_a = jnp.exp(peak_a - peak)
    factor_b = jnp.exp(peak_b - peak)
    return (
        peak,
        den_a * factor_a + den_b * factor_b,
        acc_a * factor_a[..., None] + acc_b * factor_b[..., None],
    )


def own_heads(array, start, count, axis):
    return lax.dynamic_slice_in_dim(array, start, count, axis)


def cross_local(db_keys, cross_query, neighbour_ids, index, scale):
    entries, tokens, width = db_keys.shape
    heads = width // DH
    rows = cross_query.shape[0]
    local_ids = index * entries + lax.broadcasted_iota(jnp.int32, (1, 1, entries), 2)
    counts = jnp.sum((neighbour_ids[:, :, None] == local_ids).astype(jnp.float32), axis=1)
    db_key_heads = db_keys.reshape(entries, tokens, heads, DH)
    cross_heads = cross_query.reshape(rows, heads, DH)
    cross_scores = (
        jnp.einsum("bhd,ethd->bhet", cross_heads, db_key_heads, preferred_element_type=jnp.float32)
        * scale
    )
    chosen = (counts > 0.0)[:, None, :, None]
    cross_scores = jnp.where(chosen, cross_scores, NEG)
    return (cross_scores, chosen, counts)


def cross_partial(cross_scores, chosen, counts, cross_peak, db_values):
    entries, tokens, width = db_values.shape
    heads = width // DH
    db_value_heads = db_values.reshape(entries, tokens, heads, DH)
    cross_weights = (
        jnp.where(chosen, jnp.exp(cross_scores - cross_peak[:, :, None, None]), 0.0)
        * counts[:, None, :, None]
    )
    cross_den = jnp.sum(cross_weights, axis=(2, 3))
    cross_acc = jnp.einsum(
        "bhet,ethd->bhd",
        cross_weights.astype(jnp.bfloat16),
        db_value_heads,
        preferred_element_type=jnp.float32,
    )
    return (cross_den, cross_acc)


def on_device(
    self_query,
    new_key,
    new_value,
    cache_keys,
    cache_values,
    lengths,
    db_keys,
    db_values,
    cross_query,
    neighbour_ids,
):
    scale = DH ** (-0.5)
    parts = lax.axis_size("seq")
    index = lax.axis_index("seq")
    rows, positions, width = cache_keys.shape
    heads = width // DH
    owned = heads // parts
    first = index * owned
    query_heads = self_query.reshape(rows, heads, DH)
    key_heads = cache_keys.reshape(rows, positions, heads, DH)
    value_heads = cache_values.reshape(rows, positions, heads, DH)
    scores = (
        jnp.einsum("bhd,bphd->bhp", query_heads, key_heads, preferred_element_type=jnp.float32)
        * scale
    )
    place = index * positions + lax.broadcasted_iota(jnp.int32, (rows, heads, positions), 2)
    live = place < lengths[:, None, None]
    scores = jnp.where(live, scores, NEG)
    local_peak = jnp.max(scores, axis=2)
    joined = False
    weights = jnp.where(live, jnp.exp(scores - local_peak[..., None]), 0.0)
    acc = jnp.einsum(
        "bhp,bphd->bhd",
        weights.astype(jnp.bfloat16),
        value_heads,
        preferred_element_type=jnp.float32,
    )
    den = jnp.sum(weights, axis=2)
    peak, den, acc = joined_2((local_peak, den, acc), "seq", blend)
    peak = own_heads(peak, first, owned, 1)
    den = own_heads(den, first, owned, 1)
    acc = own_heads(acc, first, owned, 1)
    query_own = (
        own_heads(self_query, first * DH, owned * DH, 1)
        .astype(jnp.float32)
        .reshape(rows, owned, DH)
    )
    key_own = (
        own_heads(new_key, first * DH, owned * DH, 1).astype(jnp.float32).reshape(rows, owned, DH)
    )
    value_own = (
        own_heads(new_value, first * DH, owned * DH, 1).astype(jnp.float32).reshape(rows, owned, DH)
    )
    score_own = jnp.sum(query_own * key_own, axis=2) * scale
    top = jnp.maximum(peak, score_own)
    factor = jnp.exp(peak - top)
    weight_own = jnp.exp(score_own - top)
    numer = (
        acc * factor[..., None]
        + weight_own.astype(jnp.bfloat16).astype(jnp.float32)[..., None] * value_own
    )
    self_out = (
        (numer / (den * factor + weight_own)[..., None])
        .reshape(rows, owned * DH)
        .astype(jnp.bfloat16)
    )
    cross_scores, chosen, counts = cross_local(db_keys, cross_query, neighbour_ids, index, scale)
    cross_peak = jnp.max(cross_scores, axis=(2, 3))
    cross_den, cross_acc = cross_partial(cross_scores, chosen, counts, cross_peak, db_values)
    cross_peak, cross_den, cross_acc = joined_2((cross_peak, cross_den, cross_acc), "seq", blend)
    cross_den = own_heads(cross_den, first, owned, 1)
    cross_acc = own_heads(cross_acc, first, owned, 1)
    cross_out = (cross_acc / cross_den[..., None]).reshape(rows, owned * DH).astype(jnp.bfloat16)
    return (self_out, cross_out)


def solution(mesh):
    in_specs = (
        P("groups", None),
        P("groups", None),
        P("groups", None),
        P("groups", "seq", None),
        P("groups", "seq", None),
        P("groups"),
        P(("groups", "seq"), None, None),
        P(("groups", "seq"), None, None),
        P("groups", None),
        P("groups", None),
    )
    out_specs = (P("groups", "seq"), P("groups", "seq"))
    return jax.shard_map(
        on_device, mesh=mesh, in_specs=in_specs, out_specs=out_specs, check_vma=False
    )
```

profile of v0, /device:TPU:0, one launch (start us, length us, event | category | flops | bytes accessed | tf_op | source)
XLA Modules:
  0.0 161.7 jit_solution(14012600609980269282)
XLA Ops:
  7.2 3.7 %copy.75 = bf16[16,8,64,128]{3,2,1,0:T(8,128)(2,1)} copy(bf16[16,8,64,128]{3,1,2,0:T(8,128)(2,1)} %bitcast.106) | data formatting | bytes 4194304
  12.5 1.9 %fusion.58 = (f32[8,64]{0,1:T(8,128)S(1)}, f32[8,64,1,128]{3,0,1,2:T(8,128)S(1)}) fusion(bf16[8,8192]{1,0:T(8,128)(2,1)S(1)} %copy-done, bf16[128,64,128]{2,1,0:T(8,128)(2,1)S(1)} %bitcast.108, pred[8]{0:T(512)(128)(4,1)S(1)} %broadcast_compare_fusion), kind=kOutput, calls=%fused_computation.73 | convolution fusion | flops 16973312 | bytes 2492424 | tf_op jit(solution)/shard_map/bhd,ethd->bhet/dot_general | solution.py:48
  14.4 2.6 %fusion.23 = f32[8,64,128]{2,0,1:T(8,128)} fusion(bf16[128,64,128]{2,1,0:T(8,128)(2,1)S(1)} %bitcast.105, f32[8,64,1,128]{3,0,1,2:T(8,128)S(1)} %get-tuple-element.439, f32[8]{0:T(128)S(1)} %fusion.53, f32[8,64]{0,1:T(8,128)S(1)} %get-tuple-element.438, pred[8]{0:T(512)(128)(4,1)S(1)} %broadcast_compare_fusion), kind=kOutput, calls=%fused_computation.30 | convolution fusion | flops 17039360 | bytes 2623528 | tf_op jit(solution)/shard_map/bhet,ethd->bhd/dot_general | solution.py:65
  17.1 7.8 %fusion.10 = f32[8,64,1,64]{3,2,1,0:T(1,128)S(1)} fusion(bf16[8,64,128,1]{2,0,1,3:T(8,128)(2,1)S(1)} %bitcast.120, bf16[8,64,8192]{2,1,0:T(8,128)(2,1)} %param.17), kind=kOutput, calls=%fused_computation.21 | convolution fusion | flops 8388608 | bytes 8650752 | tf_op jit(solution)/shard_map/bhd,bphd->bhp/dot_general | solution.py:97
  25.5 6.6 %fusion.7 = f32[8,64,1,128]{3,2,1,0:T(1,128)} fusion(bf16[8,64,64,1]{2,1,0,3:T(8,128)(2,1)S(1)} %get-tuple-element.435, bf16[8,64,8192]{2,1,0:T(8,128)(2,1)} %param.18), kind=kOutput, calls=%fused_computation.18 | convolution fusion | flops 8388608 | bytes 8716288 | tf_op jit(solution)/shard_map/bhp,bphd->bhd/dot_general | solution.py:106
  32.4 23.6 %all-gather = f32[128,64]{1,0:T(8,128)S(1)} all-gather(f32[8,64]{1,0:T(8,128)S(1)} %fusion.34), channel_id=2, replica_groups=mesh['groups'=2,'seq'=16] {'seq'}, dimensions={0}, use_global_device_ids=true | all-gather | bytes 34816 | tf_op jit(solution)/shard_map/all_gather | solution.py:13
  56.0 17.9 %all-gather.3 = f32[128,64]{1,0:T(8,128)S(1)} all-gather(f32[8,64]{1,0:T(8,128)S(1)} %copy.60), channel_id=5, replica_groups=mesh['groups'=2,'seq'=16] {'seq'}, dimensions={0}, use_global_device_ids=true | all-gather | bytes 34816 | tf_op jit(solution)/shard_map/all_gather | solution.py:13
  74.0 19.2 %all-gather.4 = f32[128,64]{1,0:T(8,128)S(1)} all-gather(f32[8,64]{1,0:T(8,128)S(1)} %copy.61), channel_id=6, replica_groups=mesh['groups'=2,'seq'=16] {'seq'}, dimensions={0}, use_global_device_ids=true | all-gather | bytes 34816 | tf_op jit(solution)/shard_map/all_gather | solution.py:13
  93.2 18.0 %all-gather.1 = f32[128,64]{1,0:T(8,128)S(1)} all-gather(f32[8,64]{1,0:T(8,128)S(1)} %get-tuple-element.436), channel_id=3, replica_groups=mesh['groups'=2,'seq'=16] {'seq'}, dimensions={0}, use_global_device_ids=true | all-gather | bytes 34816 | tf_op jit(solution)/shard_map/all_gather | solution.py:13
  113.8 19.3 %while.39 = (s32[]{:T(128)}, f32[8,64]{1,0:T(8,128)S(1)}, f32[8,64]{1,0:T(8,128)S(1)}, f32[8,64,128]{2,1,0:T(8,128)S(1)}, f32[16,8,64]{2,1,0:T(8,128)S(1)}, /*in...) while((s32[]{:T(128)}, f32[8,64]{1,0:T(8,128)S(1)}, ...), condition=%wide.region_9.10_spmd, body=%wide.region_8.9_spmd.sunk | while | flops 199685 | bytes 1331351 | solution.py:19
  134.1 18.9 %while.38 = (s32[]{:T(128)}, f32[8,64]{1,0:T(8,128)S(1)}, f32[8,64]{1,0:T(8,128)S(1)}, f32[8,64,128]{2,1,0:T(8,128)S(1)}, f32[16,8,64]{2,1,0:T(8,128)S(1)}, /*in...) while((s32[]{:T(128)}, f32[8,64]{1,0:T(8,128)S(1)}, ...), condition=%wide.region_3.4_spmd, body=%wide.region_2.3_spmd.sunk | while | flops 199685 | bytes 807063 | solution.py:19
  134.2 1.2 fusion.66
  135.4 1.2 fusion.66
  136.7 1.2 fusion.66
  138.0 1.2 fusion.66
  139.2 1.2 fusion.66
  140.5 1.2 fusion.66
  141.7 1.2 fusion.66
  143.0 1.2 fusion.66
  144.3 1.2 fusion.66
  145.5 1.2 fusion.66
  146.8 1.2 fusion.66
  148.0 1.2 fusion.66
  151.8 1.2 fusion.66
  (109 shorter events, 29.4 us)
Async XLA Ops:
  7.2 4.4 %copy-start = (bf16[8,8192]{1,0:T(8,128)(2,1)S(1)}, bf16[8,8192]{1,0:T(8,128)(2,1)}, u32[]{:S(2)}) copy-start(bf16[8,8192]{1,0:T(8,128)(2,1)} %param.22) | copy-start | bytes 393220
  7.2 3.8 %copy-start.4 = (s32[8,2]{0,1:T(2,128)S(1)}, s32[8,2]{0,1:T(2,128)}, u32[]{:S(2)}) copy-start(s32[8,2]{0,1:T(2,128)} %param.23) | copy-start | bytes 196
  7.2 3.8 %copy-start.1 = (bf16[1,128,8192]{2,1,0:T(8,128)(2,1)S(1)}, bf16[1,128,8192]{2,1,0:T(8,128)(2,1)}, u32[]{:S(2)}) copy-start(bf16[1,128,8192]{2,1,0:T(8,128)(2,1)} %param.21) | copy-start | bytes 6291460
  7.2 105.5 %all-gather.11.cloned.1.call-start = ((), (), s32[]{:S(2)}) async-start(), calls=%async_computation.1 | async-start | bytes 4456448 | tf_op jit(solution)/shard_map/all_gather | solution.py:13
  10.9 1.6 copy-start.2
  11.0 6.1 %copy-start.5 = (bf16[8,8192]{1,0:T(8,128)(2,1)S(1)}, bf16[8,8192]{1,0:T(8,128)(2,1)}, u32[]{:S(2)}) copy-start(bf16[8,8192]{1,0:T(8,128)(2,1)} %param.14) | copy-start | bytes 393220
  17.1 116.1 %all-gather.9.cloned.1.call-start = ((), (), s32[]{:S(2)}) async-start(), calls=%async_computation | async-start | bytes 4456448 | tf_op jit(solution)/shard_map/all_gather | solution.py:13
  17.1 7.8 %copy-start.3 = (s32[8]{0:T(128)S(1)}, s32[8]{0:T(128)}, u32[]{:S(2)}) copy-start(s32[8]{0:T(128)} %param.19) | copy-start | bytes 100
Sparse Core Ops, SparseCore 0:
  17.2 55.6 all-gather.10
  75.0 49.2 all-gather.8
where the time goes:
time: 163 us; the launch traced here: 162 us
  blocking collectives  78.7 us (48%)
  other arithmetic  25.1 us (15%)
  local copies, waits for them, and re-layouts  23.7 us (15%)
  matrix products  18.9 us (12%)
  between operations  14.2 us (9%)
    all_gather x4, blocking collectives, joined_2(): everything = jax.tree.map(lambda part: lax.all_gather(part, axis), shard)  78.7 us
    add x30, other arithmetic, blend(): acc_a * factor_a[..., None] + acc_b * factor_b[..., None]  22.2 us
    dynamic_slice x15, local copies, waits for them, and re-layouts, turn(): return combine(so_far, jax.tree.map(lambda part: part[k], everything))  14.6 us
    dot_general x1, matrix products, on_device(): jnp.einsum('bhd,bphd->bhp', query_heads, key_heads, preferred_element_typ...  7.81 us
    dot_general x1, matrix products, on_device(): jnp.einsum('bhp,bphd->bhd', weights.astype(jnp.bfloat16), value_heads, pr...  6.61 us
    unnamed x16, local copies, waits for them, and re-layouts  6.44 us
  transfers between devices with their start and end apart: 2, of which 0 were waited for; matrix products, arithmetic and copies ran while one was open for 23% of the time, Pallas kernels for 0%

commit v1 on v0

v1 whole, which is shorter than its diff:
```python
import functools

import jax
import jax.numpy as jnp
from jax import lax
from jax.experimental import pallas as pl
from jax.experimental.pallas import tpu as pltpu
from jax.sharding import PartitionSpec as P

DH = 128
NEG = -1e30
FLOOR = -1e29
MESH = pl.DeviceIdType.MESH


def offset_of(step, count):
    return count // 2 + ((step + 1) // 2) * (1 - 2 * (step % 2))


def pair_queries(block):
    rows = block.shape[0]
    both = jnp.concatenate([block, block], axis=0)
    row = lax.broadcasted_iota(jnp.int32, both.shape, 0)
    lane = lax.broadcasted_iota(jnp.int32, both.shape, 1)
    return jnp.where((row < rows) == (lane < DH), both, 0.0).astype(jnp.bfloat16)


def attend(query, keys, values, bias, counts):
    scores = lax.dot_general(
        query, keys, (((1,), (1,)), ((), ())), preferred_element_type=jnp.float32
    )
    scores = scores * (DH ** (-0.5)) + bias
    peak = jnp.maximum(jnp.max(scores, axis=1, keepdims=True), FLOOR)
    weights = jnp.exp(scores - peak)
    if counts is not None:
        weights = weights * counts
    den = jnp.maximum(jnp.sum(weights, axis=1, keepdims=True), 0.5)
    acc = jnp.dot(weights.astype(jnp.bfloat16), values, preferred_element_type=jnp.float32)
    return peak + jnp.log(den), acc * (1.0 / den)


def kernel(
    parts,
    group,
    lengths,
    ids,
    self_query,
    new_key,
    new_value,
    cache_keys,
    cache_values,
    db_keys,
    db_values,
    cross_query,
    self_out,
    cross_out,
    keys,
    values,
    dkeys,
    dvalues,
    squery,
    cquery,
    nkey,
    nvalue,
    bias,
    cbias,
    ccounts,
    outbox,
    inbox,
    stats,
    stream_sem,
    small_sem,
    send_sem,
    recv_sem,
):
    me = lax.axis_index("seq")
    rows, positions, width = cache_keys.shape
    entries, tokens, _ = db_keys.shape
    span = width // parts
    pairs = span // (2 * DH)
    columns = 2 * pairs

    def target(step):
        return lax.rem(me + offset_of(step, parts), parts)

    def lanes_of(device):
        return pl.ds(pl.multiple_of(device * span, span), span)

    def streams(step):
        lanes = lanes_of(target(step))
        return [
            pltpu.make_async_copy(source.at[:, :, lanes], dest.at[step], stream_sem.at[k, step])
            for k, (source, dest) in enumerate(
                (
                    (cache_keys, keys),
                    (cache_values, values),
                    (db_keys, dkeys),
                    (db_values, dvalues),
                )
            )
        ]

    def message(step):
        return pltpu.make_async_remote_copy(
            src_ref=outbox.at[step],
            dst_ref=inbox.at[step],
            send_sem=send_sem.at[step],
            recv_sem=recv_sem.at[step],
            device_id={"seq": target(step)},
            device_id_type=MESH,
        )

    own = lanes_of(me)
    small = [
        pltpu.make_async_copy(self_query, squery, small_sem.at[0]),
        pltpu.make_async_copy(cross_query, cquery, small_sem.at[1]),
        pltpu.make_async_copy(new_key.at[:, own], nkey, small_sem.at[2]),
        pltpu.make_async_copy(new_value.at[:, own], nvalue, small_sem.at[3]),
    ]
    small[0].start()
    small[1].start()

    def launch(step, carry):
        for copy in streams(step):
            copy.start()
        return carry

    lax.fori_loop(0, parts, launch, 0)
    small[2].start()
    small[3].start()

    barrier = pltpu.get_barrier_semaphore()

    def greet(step, carry):
        pl.semaphore_signal(
            barrier, inc=1, device_id={"seq": target(step)}, device_id_type=MESH
        )
        return carry

    lax.fori_loop(0, parts - 1, greet, 0)

    shape = (2 * rows, rows * positions)
    row = lax.broadcasted_iota(jnp.int32, shape, 0)
    row = jnp.where(row >= rows, row - rows, row)
    lane = lax.broadcasted_iota(jnp.int32, shape, 1)
    table = jnp.full(shape, NEG, jnp.float32)
    for b in range(rows):
        left = jnp.clip(lengths[b] - me * positions, 0, positions)
        live = (row == b) & (lane >= b * positions) & (lane < b * positions + left)
        table = jnp.where(live, 0.0, table)
    bias[...] = table
    shape = (2 * rows, entries * tokens)
    row = lax.broadcasted_iota(jnp.int32, shape, 0)
    row = jnp.where(row >= rows, row - rows, row)
    lane = lax.broadcasted_iota(jnp.int32, shape, 1)
    table = jnp.zeros(shape, jnp.float32)
    for b in range(rows):
        for e in range(entries):
            here = (row == b) & (lane >= e * tokens) & (lane < (e + 1) * tokens)
            for j in range(ids.shape[1]):
                match = here & (jnp.full(shape, ids[b, j], jnp.int32) == me * entries + e)
                table = jnp.where(match, table + 1.0, table)
    ccounts[...] = table
    cbias[...] = jnp.where(table > 0.0, 0.0, NEG)

    small[0].wait()
    small[1].wait()
    tag = lax.broadcasted_iota(jnp.int32, (2 * rows, DH), 1)

    def compute(step):
        device = target(step)
        found = [None] * columns
        sums = []
        for pair in range(pairs):
            lanes = pl.ds(pl.multiple_of(device * span, span) + pair * 2 * DH, 2 * DH)
            piece = slice(pair * 2 * DH, (pair + 1) * 2 * DH)
            found[pair], acc = attend(
                pair_queries(squery[:, lanes].astype(jnp.float32)),
                keys[step, :, :, piece].reshape(rows * positions, 2 * DH),
                values[step, :, :, piece].reshape(rows * positions, 2 * DH),
                bias[...],
                None,
            )
            found[pairs + pair], cacc = attend(
                pair_queries(cquery[:, lanes].astype(jnp.float32)),
                dkeys[step, :, :, piece].reshape(entries * tokens, 2 * DH),
                dvalues[step, :, :, piece].reshape(entries * tokens, 2 * DH),
                cbias[...],
                ccounts[...],
            )
            sums.append(jnp.concatenate([acc[:rows, :DH], cacc[:rows, :DH]], axis=0))
            sums.append(jnp.concatenate([acc[rows:, DH:], cacc[rows:, DH:]], axis=0))
        for head, part in enumerate(sums):
            outbox[step, :, head * DH : (head + 1) * DH] = part.astype(jnp.bfloat16)
        level = jnp.zeros((2 * rows, DH), jnp.float32)
        for k in range(3 * columns):
            level = jnp.where(tag == k, found[k % columns], level)
        high = level.astype(jnp.bfloat16).astype(jnp.float32)
        rest = level - high
        middle = rest.astype(jnp.bfloat16).astype(jnp.float32)
        low = rest - middle
        level = jnp.where(tag < columns, high, jnp.where(tag < 2 * columns, middle, low))
        outbox[step, :, span:] = level.astype(jnp.bfloat16)

    def block(first, count, wait_barrier, sends):
        for j in range(count):
            for copy in streams(first + j):
                copy.wait()
        for j in range(count):
            compute(first + j)
        if wait_barrier:
            pl.semaphore_wait(barrier, parts - 1)
        for j in range(sends):
            message(first + j).start()

    block(0, group, True, group)

    def turn(k, carry):
        block(k * group, group, False, group)
        return carry

    lax.fori_loop(1, parts // group - 1, turn, 0)
    block(parts - group, group, False, group - 1)

    small[2].wait()
    small[3].wait()
    query_own = squery[:, own].astype(jnp.float32)
    product = query_own * nkey[...].astype(jnp.float32)
    level_own = jnp.full((2 * rows, DH), NEG, jnp.float32)
    for pair in range(pairs):
        halves = [
            jnp.sum(product[:, h * DH : (h + 1) * DH], axis=1, keepdims=True) * (DH ** (-0.5))
            for h in (2 * pair, 2 * pair + 1)
        ]
        level_own = jnp.where(tag == pair, jnp.concatenate(halves, axis=0), level_own)

    def spread(tile, head):
        pair, half = head // 2, head % 2
        part = tile[half * rows : (half + 1) * rows]
        return jnp.concatenate(
            [
                jnp.broadcast_to(part[:, pair : pair + 1], (rows, DH)),
                jnp.broadcast_to(part[:, pairs + pair : pairs + pair + 1], (rows, DH)),
            ],
            axis=0,
        )

    def level_of(box, step):
        raw = box[step, :, span:].astype(jnp.float32)
        full = raw + pltpu.roll(raw, DH - columns, 1) + pltpu.roll(raw, DH - 2 * columns, 1)
        return jnp.where(tag < columns, full, NEG)

    level = level_of(outbox, parts - 1)
    stats[parts - 1] = level
    top = jnp.maximum(level_own, level)
    for step in range(parts - 1):
        message(step).wait_recv()
        level = level_of(inbox, step)
        stats[step] = level
        top = jnp.maximum(top, level)
    share = jnp.exp(level_own - top)
    total = share
    zero = jnp.zeros((rows, DH), jnp.float32)
    sums = [
        jnp.concatenate([nvalue[:, h * DH : (h + 1) * DH].astype(jnp.float32), zero], axis=0)
        * spread(share, h)
        for h in range(2 * pairs)
    ]
    for step in range(parts):
        box = inbox if step < parts - 1 else outbox
        share = jnp.exp(stats[step] - top)
        total = total + share
        for h in range(2 * pairs):
            part = box[step, :, h * DH : (h + 1) * DH].astype(jnp.float32)
            sums[h] = sums[h] + part * spread(share, h)
    inverse = 1.0 / total
    for h in range(2 * pairs):
        result = sums[h] * spread(inverse, h)
        self_out[:, h * DH : (h + 1) * DH] = result[:rows].astype(jnp.bfloat16)
        cross_out[:, h * DH : (h + 1) * DH] = result[rows:].astype(jnp.bfloat16)

    def drain(step, carry):
        message(step).wait_send()
        return carry

    lax.fori_loop(0, parts - 1, drain, 0)


def on_device(
    self_query,
    new_key,
    new_value,
    cache_keys,
    cache_values,
    lengths,
    db_keys,
    db_values,
    cross_query,
    neighbour_ids,
):
    parts = lax.axis_size("seq")
    rows, positions, width = cache_keys.shape
    entries, tokens, _ = db_keys.shape
    span = width // parts
    group = max(1, 2048 // span)
    half = jnp.bfloat16
    anywhere = pl.BlockSpec(memory_space=pl.ANY)
    scalar = pl.BlockSpec(memory_space=pltpu.SMEM)
    vmem = pl.BlockSpec(memory_space=pltpu.VMEM)
    out = jax.ShapeDtypeStruct((rows, span), half)
    return pl.pallas_call(
        functools.partial(kernel, parts, group),
        out_shape=(out, out),
        in_specs=[scalar, scalar] + [anywhere] * 8,
        out_specs=(vmem, vmem),
        scratch_shapes=[
            pltpu.VMEM((parts, rows, positions, span), half),
            pltpu.VMEM((parts, rows, positions, span), half),
            pltpu.VMEM((parts, entries, tokens, span), half),
            pltpu.VMEM((parts, entries, tokens, span), half),
            pltpu.VMEM((rows, width), half),
            pltpu.VMEM((rows, width), half),
            pltpu.VMEM((rows, span), half),
            pltpu.VMEM((rows, span), half),
            pltpu.VMEM((2 * rows, rows * positions), jnp.float32),
            pltpu.VMEM((2 * rows, entries * tokens), jnp.float32),
            pltpu.VMEM((2 * rows, entries * tokens), jnp.float32),
            pltpu.VMEM((parts, 2 * rows, span + DH), half),
            pltpu.VMEM((parts, 2 * rows, span + DH), half),
            pltpu.VMEM((parts, 2 * rows, DH), jnp.float32),
            pltpu.SemaphoreType.DMA((4, parts)),
            pltpu.SemaphoreType.DMA((4,)),
            pltpu.SemaphoreType.DMA((parts,)),
            pltpu.SemaphoreType.DMA((parts,)),
        ],
        compiler_params=pltpu.CompilerParams(
            collective_id=0, has_side_effects=True, vmem_limit_bytes=60 * 1024 * 1024
        ),
    )(
        lengths,
        neighbour_ids,
        self_query,
        new_key,
        new_value,
        cache_keys,
        cache_values,
        db_keys,
        db_values,
        cross_query,
    )


def solution(mesh):
    in_specs = (
        P("groups", None),
        P("groups", None),
        P("groups", None),
        P("groups", "seq", None),
        P("groups", "seq", None),
        P("groups"),
        P(("groups", "seq"), None, None),
        P(("groups", "seq"), None, None),
        P("groups", None),
        P("groups", None),
    )
    out_specs = (P("groups", "seq"), P("groups", "seq"))
    return jax.shard_map(
        on_device, mesh=mesh, in_specs=in_specs, out_specs=out_specs, check_vma=False
    )
```

time: 163 us -> 27.8 us (0.17)
  blocking collectives: 78.7 us -> 0 us
  other arithmetic: 25.1 us -> 0 us
  Pallas kernels: 0 us -> 22.9 us
  local copies, waits for them, and re-layouts: 23.7 us -> 3.94 us
  matrix products: 18.9 us -> 0 us
  between operations: 14.2 us -> 0.64 us
    all_gather x4 -> x0, blocking collectives: 78.7 us -> none  [joined_2(): everything = jax.tree.map(lambda part: lax.all_gather(part, axis), shard)]
    pallas_call x0 -> x1, Pallas kernels: none -> 22.9 us  [on_device(): pl.pallas_call(functools.partial(kernel, parts, group), out_shape=(out, o...]
    add x62 -> x0, other arithmetic: 22.7 us -> none  [the longest x30 22.2 us: blend(): acc_a * factor_a[..., None] + acc_b * factor_b[..., None]]
    dot_general x4 -> x0, matrix products: 18.9 us -> none  [the longest x1 7.81 us: on_device(): jnp.einsum('bhd,bphd->bhp', query_heads, key_heads, preferred_element_typ...]
    dynamic_slice x16 -> x0, local copies, waits for them, and re-layouts: 14.7 us -> none  [the longest x15 14.6 us: turn(): return combine(so_far, jax.tree.map(lambda part: part[k], everything))]
    unnamed x16 -> x3, local copies, waits for them, and re-layouts: 6.44 us -> 3.94 us
    slice x6 -> x0, local copies, waits for them, and re-layouts: 1.94 us -> none  [joined_2(): initial = jax.tree.map(lambda part: part[0], everything)]
  transfers between devices with their start and end apart: 2 -> 0, of which waited for: 0 -> 0; matrix products, arithmetic and copies ran while one was open for 23% -> 0% of each run, Pallas kernels for 0% -> 0%
where the time goes in v1:
time: 27.8 us; the launch traced here: 27.5 us
  Pallas kernels  22.9 us (82%)
  local copies, waits for them, and re-layouts  3.94 us (14%)
  between operations  0.64 us (2%)
    pallas_call x1, Pallas kernels, on_device(): pl.pallas_call(functools.partial(kernel, parts, group), out_shape=(out, o...  22.9 us
    unnamed x3, local copies, waits for them, and re-layouts  3.94 us

profile of v1, /device:TPU:0, one launch (start us, length us, event | category | flops | bytes accessed | tf_op | source)
XLA Modules:
  0.0 27.5 jit_solution(73825424910175453)
XLA Ops:
  0.6 1.3 %copy.12.ids = s32[8,2]{1,0:T(8,128)} copy(s32[8,2]{0,1:T(2,128)} %param.19) | data formatting | bytes 128 | tf_op args[9]
  2.0 22.9 %shard_map.113 = (bf16[8,512]{1,0:T(8,128)(2,1)}, bf16[8,512]{1,0:T(8,128)(2,1)}) custom-call(s32[8]{0:T(128)} %lengths.1, s32[8,2]{1,0:T(8,128)} %copy.12.ids, bf16[8,8192]{1,0:T(8,128)(2,1)} %self_query.1, bf16[8,8192]{1,0:T(8,128)(2,1)} %new_key.1, bf16[8,8192]{1,0:T(8,128)(2,1)} %new_value.1, bf16[8,64,8192]{2,1,0:T(8,128)(2,1)} %cache_keys.1, ...), custom_call_target="tpu_custom_call" | custom-call | tf_op jit(solution)/shard_map/pallas_call | solution.py:311
  24.9 1.3 %copy.15 = bf16[8,512]{1,0:T(8,128)(2,1)} copy(bf16[8,512]{1,0:T(8,128)(2,1)} %get-tuple-element.4) | data formatting | bytes 16384
  26.2 1.3 %copy.16 = bf16[8,512]{1,0:T(8,128)(2,1)} copy(bf16[8,512]{1,0:T(8,128)(2,1)} %get-tuple-element.5) | data formatting | bytes 16384

commit v2 on v1

v2 whole, which is shorter than its diff:
```python
import functools

import jax
import jax.numpy as jnp
from jax import lax
from jax.experimental import pallas as pl
from jax.experimental.pallas import tpu as pltpu
from jax.sharding import PartitionSpec as P

DH = 128
NEG = -1e30
FLOOR = -1e29
MESH = pl.DeviceIdType.MESH


def offset_of(step, count):
    return count // 2 + ((step + 1) // 2) * (1 - 2 * (step % 2))


def spread_queries(block, first, total):
    rows, width = block.shape
    zero = jnp.zeros((rows, DH), block.dtype)
    heads = width // DH
    return jnp.concatenate(
        [
            jnp.concatenate(
                [
                    block[:, h * DH : (h + 1) * DH] if first + h == i else zero
                    for h in range(heads)
                ],
                axis=1,
            )
            for i in range(total)
        ],
        axis=0,
    ).astype(jnp.bfloat16)


def weigh(queries, keys, bias, counts):
    scores = sum(
        lax.dot_general(k, q, (((1,), (1,)), ((), ())), preferred_element_type=jnp.float32)
        for q, k in zip(queries, keys)
    )
    scores = scores.T * (DH ** (-0.5)) + jnp.concatenate([bias] * (scores.shape[1] // bias.shape[0]))
    peak = jnp.maximum(jnp.max(scores, axis=1, keepdims=True), FLOOR)
    weights = jnp.exp(scores - peak)
    if counts is not None:
        weights = weights * jnp.concatenate([counts] * (scores.shape[0] // counts.shape[0]))
    den = jnp.maximum(jnp.sum(weights, axis=1, keepdims=True), 0.5)
    return weights.astype(jnp.bfloat16), 1.0 / den, peak + jnp.log(den)


def kernel(
    parts,
    ahead,
    lengths_in,
    ids_in,
    self_query,
    new_key,
    new_value,
    cache_keys,
    cache_values,
    db_keys,
    db_values,
    cross_query,
    out,
    lengths,
    ids,
    keys,
    values,
    dkeys,
    dvalues,
    squery,
    cquery,
    nkey,
    nvalue,
    bias,
    cbias,
    ccounts,
    outbox,
    sidebox,
    merged,
    inbox,
    stats,
    stream_sem,
    small_sem,
    send_sem,
    recv_sem,
    side_send,
    side_recv,
):
    me = lax.axis_index("seq")
    rows, positions, width = cache_keys.shape
    entries, tokens, _ = db_keys.shape
    span = width // parts
    pairs = span // (2 * DH)
    columns = 2 * pairs

    chips = parts // 2
    core = lax.rem(me, 2)
    chip = me // 2
    partner = chip * 2 + 1 - core

    def peer(step):
        return lax.rem(chip + offset_of(step, chips), chips) * 2 + core

    def target(k):
        flip = 1 - lax.rem(k, 2)
        return peer(k // 2) - core + core * (1 - flip) + (1 - core) * flip

    def lanes_of(device):
        return pl.ds(pl.multiple_of(device * span, span), span)

    def streams(step):
        lanes = lanes_of(target(step))
        return [
            pltpu.make_async_copy(source.at[:, :, lanes], dest.at[step], stream_sem.at[k, step])
            for k, (source, dest) in enumerate(
                (
                    (cache_keys, keys),
                    (cache_values, values),
                    (db_keys, dkeys),
                    (db_values, dvalues),
                )
            )
        ]

    def handover(step):
        return pltpu.make_async_remote_copy(
            src_ref=outbox.at[2 * step],
            dst_ref=sidebox.at[step],
            send_sem=side_send.at[step],
            recv_sem=side_recv.at[step],
            device_id={"seq": partner},
            device_id_type=MESH,
        )

    def message(step):
        return pltpu.make_async_remote_copy(
            src_ref=merged.at[step],
            dst_ref=inbox.at[step],
            send_sem=send_sem.at[step],
            recv_sem=recv_sem.at[step],
            device_id={"seq": peer(step)},
            device_id_type=MESH,
        )

    own = lanes_of(me)
    small = [
        pltpu.make_async_copy(self_query, squery, small_sem.at[0]),
        pltpu.make_async_copy(cross_query, cquery, small_sem.at[1]),
        pltpu.make_async_copy(new_key.at[:, own], nkey, small_sem.at[2]),
        pltpu.make_async_copy(new_value.at[:, own], nvalue, small_sem.at[3]),
    ]
    scalars = [
        pltpu.make_async_copy(lengths_in, lengths, small_sem.at[4]),
        pltpu.make_async_copy(ids_in, ids, small_sem.at[5]),
    ]
    for copy in small[:2] + scalars:
        copy.start()

    def launch(step, carry):
        for copy in streams(step):
            copy.start()
        return carry

    lax.fori_loop(0, 2 * ahead, launch, 0)
    small[2].start()
    small[3].start()

    barrier = pltpu.get_barrier_semaphore()

    def greet(step, carry):
        pl.semaphore_signal(
            barrier, inc=1, device_id={"seq": peer(step)}, device_id_type=MESH
        )
        return carry

    lax.fori_loop(0, chips - 1, greet, 0)
    pl.semaphore_signal(barrier, inc=1, device_id={"seq": partner}, device_id_type=MESH)

    for copy in scalars:
        copy.wait()
    shape = (2 * rows, rows * positions)
    row = lax.broadcasted_iota(jnp.int32, shape, 0)
    row = jnp.where(row >= rows, row - rows, row)
    lane = lax.broadcasted_iota(jnp.int32, shape, 1)
    table = jnp.full(shape, NEG, jnp.float32)
    for b in range(rows):
        left = jnp.clip(lengths[b] - me * positions, 0, positions)
        live = (row == b) & (lane >= b * positions) & (lane < b * positions + left)
        table = jnp.where(live, 0.0, table)
    bias[...] = table
    shape = (2 * rows, entries * tokens)
    row = lax.broadcasted_iota(jnp.int32, shape, 0)
    row = jnp.where(row >= rows, row - rows, row)
    lane = lax.broadcasted_iota(jnp.int32, shape, 1)
    table = jnp.zeros(shape, jnp.float32)
    for b in range(rows):
        for e in range(entries):
            here = (row == b) & (lane >= e * tokens) & (lane < (e + 1) * tokens)
            for j in range(ids.shape[0]):
                match = here & (jnp.full(shape, ids[j, b], jnp.int32) == me * entries + e)
                table = jnp.where(match, table + 1.0, table)
    ccounts[...] = table
    cbias[...] = jnp.where(table > 0.0, 0.0, NEG)

    small[0].wait()
    small[1].wait()
    tag = lax.broadcasted_iota(jnp.int32, (2 * rows, DH), 1)

    def compute_both(first):
        heads = 2 * pairs
        results = []
        for source, held, extent, table, number in (
            (squery, keys, rows * positions, bias[...], None),
            (cquery, dkeys, entries * tokens, cbias[...], ccounts[...]),
        ):
            queries, blocks = [], []
            for j in range(2):
                lanes = lanes_of(target(first + j))
                block = source[:, lanes].astype(jnp.float32)
                queries.append(spread_queries(block, j * heads, 2 * heads))
                blocks.append(held[first + j].reshape(extent, span))
            results.append(weigh(queries, blocks, table, number))
        for j in range(2):
            compute(first + j, j, results)

    def compute(step, place, results):
        found = [None] * columns
        sums = []
        for pair in range(pairs):
            piece = slice(pair * 2 * DH, (pair + 1) * 2 * DH)
            at = slice((place * pairs + pair) * 2 * rows, (place * pairs + pair + 1) * 2 * rows)
            accs = []
            for kind, (held, extent) in enumerate(
                ((values, rows * positions), (dvalues, entries * tokens))
            ):
                weights, inverse, level = results[kind]
                acc = jnp.dot(
                    weights[at],
                    held[step, :, :, piece].reshape(extent, 2 * DH),
                    preferred_element_type=jnp.float32,
                )
                accs.append(acc * inverse[at])
                found[kind * pairs + pair] = level[at]
            acc, cacc = accs
            sums.append(jnp.concatenate([acc[:rows, :DH], cacc[:rows, :DH]], axis=0))
            sums.append(jnp.concatenate([acc[rows:, DH:], cacc[rows:, DH:]], axis=0))
        for head, part in enumerate(sums):
            outbox[step, :, head * DH : (head + 1) * DH] = part.astype(jnp.bfloat16)
        level = jnp.zeros((2 * rows, DH), jnp.float32)
        for k in range(3 * columns):
            level = jnp.where(tag == k, found[k % columns], level)
        outbox[step, :, span:] = packed(level)

    def spread(tile, head):
        pair, half = head // 2, head % 2
        part = tile[half * rows : (half + 1) * rows]
        return jnp.concatenate(
            [
                jnp.broadcast_to(part[:, pair : pair + 1], (rows, DH)),
                jnp.broadcast_to(part[:, pairs + pair : pairs + pair + 1], (rows, DH)),
            ],
            axis=0,
        )

    def level_of(box, step):
        raw = box[step, :, span:].astype(jnp.float32)
        full = raw + pltpu.roll(raw, DH - columns, 1) + pltpu.roll(raw, DH - 2 * columns, 1)
        return jnp.where(tag < columns, full, NEG)

    def packed(level):
        high = level.astype(jnp.bfloat16).astype(jnp.float32)
        rest = level - high
        middle = rest.astype(jnp.bfloat16).astype(jnp.float32)
        low = rest - middle
        level = jnp.where(tag < columns, high, jnp.where(tag < 2 * columns, middle, low))
        return level.astype(jnp.bfloat16)

    def merge(step):
        first, second = level_of(outbox, 2 * step + 1), level_of(sidebox, step)
        top = jnp.maximum(first, second)
        share, other = jnp.exp(first - top), jnp.exp(second - top)
        total = share + other
        inverse = 1.0 / total
        share, other = share * inverse, other * inverse
        for h in range(2 * pairs):
            piece = slice(h * DH, (h + 1) * DH)
            part = outbox[2 * step + 1, :, piece].astype(jnp.float32) * spread(share, h)
            part = part + sidebox[step, :, piece].astype(jnp.float32) * spread(other, h)
            merged[step, :, piece] = part.astype(jnp.bfloat16)
        level = top + jnp.log(total)
        level = jnp.where(tag < columns, level, 0.0)
        level = (
            level
            + jnp.where(tag < 2 * columns, pltpu.roll(level, columns, 1), 0.0)
            + pltpu.roll(level, 2 * columns, 1)
        )
        merged[step, :, span:] = packed(level)

    def block(step, fill):
        for j in range(2):
            for copy in streams(2 * step + j):
                copy.wait()
        if fill:
            for j in range(2):
                for copy in streams(2 * (step + ahead) + j):
                    copy.start()
        compute_both(2 * step)
        handover(step).start()

    def pass_on(step):
        handover(step).wait_recv()
        merge(step)
        message(step).start()

    pl.semaphore_wait(barrier, chips)
    block(0, ahead < chips)

    def turn(fill, step, carry):
        block(step, fill)
        pass_on(step - 1)
        return carry

    lax.fori_loop(1, chips - ahead, functools.partial(turn, True), 0)
    lax.fori_loop(max(1, chips - ahead), chips, functools.partial(turn, False), 0)

    small[2].wait()
    small[3].wait()
    query_own = squery[:, own].astype(jnp.float32)
    product = query_own * nkey[...].astype(jnp.float32)
    level_own = jnp.full((2 * rows, DH), NEG, jnp.float32)
    for pair in range(pairs):
        halves = [
            jnp.sum(product[:, h * DH : (h + 1) * DH], axis=1, keepdims=True) * (DH ** (-0.5))
            for h in (2 * pair, 2 * pair + 1)
        ]
        level_own = jnp.where(tag == pair, jnp.concatenate(halves, axis=0), level_own)

    boxes = [(outbox, parts - 1)] + [(inbox, step) for step in range(chips - 2)]
    boxes += [(sidebox, chips - 1), (inbox, chips - 2)]
    top = level_own
    for k, (box, step) in enumerate(boxes):
        if box is inbox:
            message(step).wait_recv()
        if box is sidebox:
            handover(step).wait_recv()
        level = level_of(box, step)
        stats[k] = level
        top = jnp.maximum(top, level)
    share = jnp.exp(level_own - top)
    total = share
    zero = jnp.zeros((rows, DH), jnp.float32)
    sums = [
        jnp.concatenate([nvalue[:, h * DH : (h + 1) * DH].astype(jnp.float32), zero], axis=0)
        * spread(share, h)
        for h in range(2 * pairs)
    ]
    for k, (box, step) in enumerate(boxes):
        share = jnp.exp(stats[k] - top)
        total = total + share
        for h in range(2 * pairs):
            part = box[step, :, h * DH : (h + 1) * DH].astype(jnp.float32)
            sums[h] = sums[h] + part * spread(share, h)
    inverse = 1.0 / total
    for h in range(2 * pairs):
        result = sums[h] * spread(inverse, h)
        out[:, h * DH : (h + 1) * DH] = result.astype(jnp.bfloat16)

    def drain(step, carry):
        message(step).wait_send()
        return carry

    lax.fori_loop(0, chips - 1, drain, 0)

    def drain_side(step, carry):
        handover(step).wait_send()
        return carry

    lax.fori_loop(0, chips, drain_side, 0)


def on_device(
    self_query,
    new_key,
    new_value,
    cache_keys,
    cache_values,
    lengths,
    db_keys,
    db_values,
    cross_query,
    neighbour_ids,
):
    parts = lax.axis_size("seq")
    rows, positions, width = cache_keys.shape
    entries, tokens, _ = db_keys.shape
    span = width // parts
    chips = parts // 2
    ahead = min(3, chips)
    half = jnp.bfloat16
    anywhere = pl.BlockSpec(memory_space=pl.ANY)
    vmem = pl.BlockSpec(memory_space=pltpu.VMEM)
    out = pl.pallas_call(
        functools.partial(kernel, parts, ahead),
        out_shape=jax.ShapeDtypeStruct((2 * rows, span), half),
        in_specs=[anywhere] * 10,
        out_specs=vmem,
        scratch_shapes=[
            pltpu.SMEM(lengths.shape, jnp.int32),
            pltpu.SMEM(neighbour_ids.shape[::-1], jnp.int32),
            pltpu.VMEM((parts, rows, positions, span), half),
            pltpu.VMEM((parts, rows, positions, span), half),
            pltpu.VMEM((parts, entries, tokens, span), half),
            pltpu.VMEM((parts, entries, tokens, span), half),
            pltpu.VMEM((rows, width), half),
            pltpu.VMEM((rows, width), half),
            pltpu.VMEM((rows, span), half),
            pltpu.VMEM((rows, span), half),
            pltpu.VMEM((2 * rows, rows * positions), jnp.float32),
            pltpu.VMEM((2 * rows, entries * tokens), jnp.float32),
            pltpu.VMEM((2 * rows, entries * tokens), jnp.float32),
            pltpu.VMEM((parts, 2 * rows, span + DH), half),
            pltpu.VMEM((chips, 2 * rows, span + DH), half),
            pltpu.VMEM((chips, 2 * rows, span + DH), half),
            pltpu.VMEM((chips, 2 * rows, span + DH), half),
            pltpu.VMEM((chips + 1, 2 * rows, DH), jnp.float32),
            pltpu.SemaphoreType.DMA((4, parts)),
            pltpu.SemaphoreType.DMA((6,)),
            pltpu.SemaphoreType.DMA((chips,)),
            pltpu.SemaphoreType.DMA((chips,)),
            pltpu.SemaphoreType.DMA((chips,)),
            pltpu.SemaphoreType.DMA((chips,)),
        ],
        compiler_params=pltpu.CompilerParams(
            collective_id=0, has_side_effects=True, vmem_limit_bytes=60 * 1024 * 1024
        ),
    )(
        lengths,
        neighbour_ids.T,
        self_query,
        new_key,
        new_value,
        cache_keys,
        cache_values,
        db_keys,
        db_values,
        cross_query,
    )
    return out[:rows], out[rows:]


def solution(mesh):
    in_specs = (
        P("groups", None),
        P("groups", None),
        P("groups", None),
        P("groups", "seq", None),
        P("groups", "seq", None),
        P("groups"),
        P(("groups", "seq"), None, None),
        P(("groups", "seq"), None, None),
        P("groups", None),
        P("groups", None),
    )
    out_specs = (P("groups", "seq"), P("groups", "seq"))
    return jax.shard_map(
        on_device, mesh=mesh, in_specs=in_specs, out_specs=out_specs, check_vma=False
    )
```

time: 27.8 us -> 24.3 us (0.87)
  local copies, waits for them, and re-layouts: 3.94 us -> 1.32 us
  Pallas kernels: 22.9 us -> 22.2 us
    unnamed x3 -> x0, local copies, waits for them, and re-layouts: 3.94 us -> none
    slice x0 -> x1, local copies, waits for them, and re-layouts: none -> 1.32 us  [on_device(): return (out[:rows], out[rows:])]
    pallas_call x1, Pallas kernels: 22.9 us -> 22.2 us  [on_device(): pl.pallas_call(functools.partial(kernel, parts, ahead), out_shape=jax.Sha...]
where the time goes in v2:
time: 24.3 us; the launch traced here: 24.1 us
  Pallas kernels  22.2 us (91%)
  local copies, waits for them, and re-layouts  1.32 us (5%)
  between operations  0.64 us (3%)
    pallas_call x1, Pallas kernels, on_device(): pl.pallas_call(functools.partial(kernel, parts, ahead), out_shape=jax.Sha...  22.2 us
    slice x1, local copies, waits for them, and re-layouts, on_device(): return (out[:rows], out[rows:])  1.32 us

profile of v2, /device:TPU:0, one launch (start us, length us, event | category | flops | bytes accessed | tf_op | source)
XLA Modules:
  0.0 24.1 jit_solution(12774421534255000268)
XLA Ops:
  0.6 22.2 %shard_map.113 = bf16[16,512]{1,0:T(8,128)(2,1)} custom-call(s32[8]{0:T(128)} %lengths_in.1, s32[2,8]{1,0:T(2,128)} %bitcast.1, bf16[8,8192]{1,0:T(8,128)(2,1)} %self_query.1, bf16[8,8192]{1,0:T(8,128)(2,1)} %new_key.1, bf16[8,8192]{1,0:T(8,128)(2,1)} %new_value.1, bf16[8,64,8192]{2,1,0:T(8,128)(2,1)} %cache_keys.1, bf16[8,64,8192]{2,1,0:T(8,128)(2,1)} %cache_values.1, ...), custom_call_target="tpu_custom_call" | custom-call | tf_op jit(solution)/shard_map/pallas_call | solution.py:405
  22.8 1.3 %fusion = (bf16[8,512]{1,0:T(8,128)(2,1)}, bf16[8,512]{1,0:T(8,128)(2,1)}) fusion(bf16[16,512]{1,0:T(8,128)(2,1)} %shard_map.113), kind=kLoop, calls=%fused_computation | loop fusion | bytes 32768 | tf_op jit(solution)/shard_map/slice | solution.py:451
